TPU v7x, 32 devices: a whole 2x2x4 slice. The times are simulated.
32 devices in a mesh: snap: 2 (over y), row: 8 (over z, x), col: 2 (over core).
Axes of the slice: x: 2, y: 2, z: 4, core: 2. Of those that a mesh axis runs over, the one named last changes fastest.
Arguments:
- density: bfloat16 [8192, 1024], P(('snap', 'row'), 'col'), parts along dimension 0, may hold values from -0.5 to 2
- pattern: int32 [256, 32], P(('snap', 'row'), 'col'), parts along dimension 0, may hold values 0 or 1
- filter_mask: int32 [256, 32], P(('snap', 'row')), parts along dimension 0, may hold values 0 or 1
Outputs:
- purified: bfloat16 [8192, 1024], P(('snap', 'row'), 'col'), parts along dimension 0
- traces: float32 [4], P('snap'), parts along dimension 0
There are 2 independent parts, one for each index of `snap`. A program takes and returns all parts, laid end to end along the dimension named above; each array names one. Nothing has to cross between parts.
All inputs are finite; a program needn't handle non-finite values. No bound on the sum of `pattern` or of `filter_mask` on one device may be relied on, other than what follows from the above.
Results may differ from a plain program's by a relative error of at most 0.006.
Values may be sent and summed in bfloat16 or wider, within the bound.
A program may use at most 64 MiB of HBM per device.

v0:
```python
import jax
import jax.numpy as jnp
from jax import lax
from jax.sharding import PartitionSpec as P

BLK = 32


def extended_2(value, sides, width):
    for axis, dim in sides:
        size, length = (lax.axis_size(axis), value.shape[dim])
        up = [(i, (i + 1) % size) for i in range(size - 1)]
        down = [(j, i) for i, j in up]
        last = lax.slice_in_dim(value, length - width, length, axis=dim)
        leading = lax.slice_in_dim(value, 0, width, axis=dim)
        before = lax.ppermute(last, axis, up)
        after = lax.ppermute(leading, axis, down)
        value = jnp.concatenate([before, value, after], axis=dim)
    return value


def valid_slots(first_row, row_count, first_slot, slot_count, half_band, block_total):
    row_index = first_row + jnp.arange(row_count, dtype=jnp.int32)
    slot_index = first_slot + jnp.arange(slot_count, dtype=jnp.int32)
    column_index = row_index[:, None] + slot_index[None, :] - half_band
    return ((column_index >= 0) & (column_index < block_total)).astype(jnp.int32)


def expand_mask(values, keep_mask):
    block_rows = keep_mask.shape[0]
    slot_count = keep_mask.shape[1]
    blocks = values.reshape(block_rows, BLK, slot_count, BLK)
    blocks = blocks * keep_mask.astype(values.dtype)[:, None, :, None]
    return blocks.reshape(block_rows * BLK, slot_count * BLK)


def shift_slots(segment, moved):
    height = segment.shape[0]
    if moved > 0:
        return jnp.concatenate(
            [
                jnp.zeros((height, moved * BLK), segment.dtype),
                segment[:, : segment.shape[1] - moved * BLK],
            ],
            1,
        )
    if moved < 0:
        return jnp.concatenate(
            [segment[:, -moved * BLK :], jnp.zeros((height, -moved * BLK), segment.dtype)], 1
        )
    return segment


def band_part(left, extended, first_slot, column_slots, slot_count, half_band):
    block_rows = left.shape[0] // BLK
    byte_limit = 4 * 1024 * 1024
    group_rows = 1
    for candidate in (8, 4, 2):
        if (
            block_rows % candidate == 0
            and candidate * slot_count * BLK * column_slots * BLK * 2 <= byte_limit
        ):
            group_rows = candidate
            break

    def one_group(group):
        first = group * group_rows
        stacked = []
        for offset in range(slot_count):
            segment = lax.dynamic_slice_in_dim(
                extended, (first + offset) * BLK, group_rows * BLK, 0
            )
            segment = shift_slots(segment, offset - half_band)
            segment = lax.dynamic_slice_in_dim(segment, first_slot * BLK, column_slots * BLK, 1)
            stacked.append(segment.reshape(group_rows, BLK, column_slots * BLK))
        gathered = jnp.stack(stacked, 1).reshape(group_rows, slot_count * BLK, column_slots * BLK)
        left_rows = lax.dynamic_slice_in_dim(left, first * BLK, group_rows * BLK, 0).reshape(
            group_rows, BLK, slot_count * BLK
        )
        result = jnp.einsum("gak,gkn->gan", left_rows, gathered, preferred_element_type=jnp.float32)
        return result.reshape(group_rows * BLK, column_slots * BLK)

    result = lax.map(one_group, jnp.arange(block_rows // group_rows, dtype=jnp.int32))
    return result.reshape(block_rows * BLK, column_slots * BLK)


def diagonal_sum(values, chosen):
    block_rows = values.shape[0] // BLK
    slot_total = values.shape[1] // BLK
    diagonal = jnp.diagonal(values.reshape(block_rows, BLK, slot_total, BLK), axis1=1, axis2=3)
    return jnp.sum(diagonal.astype(jnp.float32) * chosen[None, :, None])


def slot_products(
    full_rows, extended, own_filter, first_slot, half_slots, slot_count, half_band, collect
):
    square = band_part(full_rows, extended, first_slot, half_slots, slot_count, half_band)
    squared = expand_mask(square, own_filter).astype(jnp.bfloat16)
    squared_rows = collect(squared)
    cube = band_part(squared_rows, extended, first_slot, half_slots, slot_count, half_band)
    purified = (3.0 * squared.astype(jnp.float32) - 2.0 * expand_mask(cube, own_filter)).astype(
        jnp.bfloat16
    )
    return (purified, squared)


def per_device(density, pattern, filter_mask):
    half_slots = density.shape[1] // BLK
    slot_count = 2 * half_slots
    block_rows = density.shape[0] // BLK
    col_id = lax.axis_index("col")
    row_id = lax.axis_index("row")
    block_total = block_rows * lax.axis_size("row")
    first_slot = col_id * half_slots
    own_valid = valid_slots(
        row_id * block_rows, block_rows, first_slot, half_slots, half_slots, block_total
    )
    kept = expand_mask(density, pattern * own_valid)
    chosen = (first_slot + jnp.arange(half_slots, dtype=jnp.int32) == half_slots).astype(
        jnp.float32
    )
    trace_kept = diagonal_sum(kept, chosen)
    total_kept = lax.psum(trace_kept, ("row", "col"))
    own_filter = lax.dynamic_slice_in_dim(filter_mask, first_slot, half_slots, 1) * own_valid
    rim_rows = extended_2(kept, (("row", 0),), half_slots * BLK)
    extended = lax.all_gather(rim_rows, "col", axis=1, tiled=True)
    full_rows = extended[half_slots * BLK : half_slots * BLK + block_rows * BLK]

    def collect_half(squared):
        return lax.all_gather(squared, "col", axis=1, tiled=True)

    purified, squared = slot_products(
        full_rows,
        extended,
        own_filter,
        first_slot,
        half_slots,
        slot_count,
        half_slots,
        collect_half,
    )
    trace_squared = diagonal_sum(squared, chosen)
    total_squared = lax.psum(trace_squared, ("row", "col"))
    order_total = block_total * BLK
    traces = jnp.stack([total_kept, total_squared]) / order_total
    return (purified, traces)


def solution(mesh):
    return jax.shard_map(
        per_device,
        mesh=mesh,
        in_specs=(P(("snap", "row"), "col"), P(("snap", "row"), "col"), P(("snap", "row"), None)),
        out_specs=(P(("snap", "row"), "col"), P("snap")),
        check_vma=False,
    )
```

profile of v0, /device:TPU:0, one launch (start us, length us, event | category | flops | bytes accessed | tf_op | source)
XLA Modules:
  0.0 517.6 jit_solution(5589783563380693730)
XLA Ops:
  8.4 2.1 mul.804
  10.6 4.9 collective-permute-start
  15.5 1.3 collective-permute-start.1
  16.8 21.1 %collective-permute-done = bf16[512,512]{1,0:T(8,128)(2,1)S(1)} collective-permute-done((bf16[512,512]{1,0:T(8,128)(2,1)S(1)}, bf16[512,512]{1,0:T(8,128)(2,1)S(1)}, u32[]{:S(2)}, u32[]{:S(2)}) %collective-permute-start) | collective-permute-done | bytes 524320 | tf_op jit(solution)/shard_map/ppermute | solution.py:16
  37.9 1.3 pad_maximum_fusion
  39.2 1.2 reshape.769
  40.5 4.3 copy.7
  44.8 2.4 mul.808.clone
  47.2 4.7 mul.809
  51.9 1.8 all-gather.3.cloned.1.call-done
  53.7 2.3 slice.442
  56.0 1.1 broadcast.199.clone
  57.1 199.7 %while.26 = (s32[]{:T(128)}, f32[4,128,512]{2,1,0:T(8,128)}, s32[4]{0:T(128)S(1)}, bf16[512,1024]{1,0:T(8,128)(2,1)}, bf16[1536,1024]{1,0:T(8,128)(2,1)}, /*inde...) while((s32[]{:T(128)}, f32[4,128,512]{2,1,0:T(8,128)}, ...), condition=%wide.region_1.2_spmd, body=%wide.region_0.1_spmd.sunk | while | flops 134217904 | bytes 56200764 | solution.py:83
  58.6 1.7 constant_dynamic-slice_fusion.65
  60.3 1.7 constant_dynamic-slice_fusion.66
  63.5 1.1 fusion.26
  65.3 1.6 constant_dynamic-update-slice_fusion.129
  66.9 1.6 constant_dynamic-update-slice_fusion.130
  68.4 1.7 constant_dynamic-slice_fusion.67
  103.3 3.0 fusion.27
  108.6 1.7 constant_dynamic-slice_fusion.65
  110.3 1.7 constant_dynamic-slice_fusion.66
  113.4 1.1 fusion.26
  115.2 1.6 constant_dynamic-update-slice_fusion.129
  116.8 1.6 constant_dynamic-update-slice_fusion.130
  118.3 1.7 constant_dynamic-slice_fusion.67
  153.2 3.0 fusion.27
  158.5 1.7 constant_dynamic-slice_fusion.65
  160.2 1.7 constant_dynamic-slice_fusion.66
  163.3 1.1 fusion.26
  165.1 1.6 constant_dynamic-update-slice_fusion.129
  166.7 1.6 constant_dynamic-update-slice_fusion.130
  168.3 1.7 constant_dynamic-slice_fusion.67
  203.1 3.0 fusion.27
  208.4 1.7 constant_dynamic-slice_fusion.65
  210.1 1.7 constant_dynamic-slice_fusion.66
  213.2 1.1 fusion.26
  215.0 1.6 constant_dynamic-update-slice_fusion.129
  216.6 1.6 constant_dynamic-update-slice_fusion.130
  218.2 1.7 constant_dynamic-slice_fusion.67
  253.0 3.0 fusion.27
  256.7 2.5 fusion.4
  259.2 4.6 multiply_bitcast_fusion
  263.8 2.8 gather_fusion
  266.7 2.7 reshape_reshape.10
  269.4 7.3 %copy.8 = f32[16,32,16,32]{2,0,3,1:T(8,128)} copy(f32[16,32,16,32]{3,2,1,0:T(8,128)} %reshape_reshape.10) | data formatting | bytes 2097152 | tf_op jit(solution)/shard_map/reshape;reshape | solution.py:32
  276.6 6.8 %fusion = bf16[16,16,32,32]{1,0,3,2:T(8,128)(2,1)} fusion(f32[16,32,16,32]{2,0,3,1:T(8,128)} %copy.8, f32[16,16]{1,0:T(8,128)S(1)} %get-tuple-element.403), kind=kLoop, calls=%fused_computation.163 | loop fusion | flops 524288 | bytes 1573888 | tf_op jit(solution)/shard_map/jit(diagonal)/transpose | solution.py:90
  283.4 2.8 gather_fusion.1
  287.0 34.8 %all-reduce.62 = (f32[1]{0:T(128)}, f32[1]{0:T(128)}) all-reduce(f32[1]{0:T(128)} %bitcast.140, f32[1]{0:T(128)} %bitcast.138), channel_id=1, replica_groups=mesh['snap'=2,'row'=8,'col'=2] {'row','col'}, use_global_device_ids=true, to_apply=%region_7.8 | all-reduce | flops 2 | bytes 16 | tf_op jit(solution)/shard_map/psum | solution.py:143
  321.9 1.8 maximum_multiply_fusion
  324.8 183.3 %while.27 = (s32[]{:T(128)}, f32[4,128,512]{2,1,0:T(8,128)}, s32[4]{0:T(128)S(1)}, bf16[512,1024]{1,0:T(8,128)(2,1)}, bf16[1536,1024]{1,0:T(8,128)(2,1)S(1)}, /*...) while((s32[]{:T(128)}, f32[4,128,512]{2,1,0:T(8,128)}, ...), condition=%wide.region_3.4_spmd, body=%wide.region_2.3_spmd.sunk | while | flops 134217904 | bytes 43617860 | solution.py:83
  329.9 1.6 constant_dynamic-update-slice_fusion.161
  331.5 1.6 constant_dynamic-update-slice_fusion.162
  366.9 3.0 fusion.31
  375.7 1.6 constant_dynamic-update-slice_fusion.161
  377.3 1.6 constant_dynamic-update-slice_fusion.162
  412.7 3.0 fusion.31
  421.5 1.6 constant_dynamic-update-slice_fusion.161
  423.1 1.6 constant_dynamic-update-slice_fusion.162
  458.5 3.0 fusion.31
  467.3 1.6 constant_dynamic-update-slice_fusion.161
  468.9 1.6 constant_dynamic-update-slice_fusion.162
  504.3 3.0 fusion.31
  508.0 2.8 fusion.3
  (694 shorter events, 299.2 us)
Async XLA Ops:
  7.2 46.5 %all-gather.3.cloned.1.call-start = ((), (), s32[]{:S(2)}) async-start(), calls=%async_computation | async-start | bytes 4718592 | tf_op jit(solution)/shard_map/all_gather | solution.py:126
  10.6 27.3 %collective-permute-start = (bf16[512,512]{1,0:T(8,128)(2,1)S(1)}, bf16[512,512]{1,0:T(8,128)(2,1)S(1)}, u32[]{:S(2)}, u32[]{:S(2)}) collective-permute-start(bf16[512,512]{1,0:T(8,128)(2,1)S(1)} %mul.805), channel_id=1, source_target_pairs={{0,2},{2,4},{4,6},{6,8},{8,10},{10,12},{12,14},{1,3},{3,5},{5,7},{... | collective-permute-start | bytes 1572872 | tf_op jit(solution)/shard_map/ppermute | solution.py:16
  15.5 22.4 %collective-permute-start.1 = (bf16[512,512]{1,0:T(8,128)(2,1)S(1)}, bf16[512,512]{1,0:T(8,128)(2,1)S(1)}, u32[]{:S(2)}, u32[]{:S(2)}) collective-permute-start(bf16[512,512]{1,0:T(8,128)(2,1)S(1)} %mul.805), channel_id=1, source_target_pairs={{2,0},{4,2},{6,4},{8,6},{10,8},{12,10},{14,12},{3,1},{5,3},{7,5},{... | collective-permute-start | bytes 1572872 | tf_op jit(solution)/shard_map/ppermute | solution.py:17
  39.2 284.5 %all-gather.5.cloned.1.call-start = ((), (), s32[]{:S(2)}) async-start(), calls=%async_computation.1 | async-start | bytes 1572864 | tf_op jit(solution)/shard_map/all_gather | solution.py:130
  57.1 13.0 %copy-start = (bf16[1536,1024]{1,0:T(8,128)(2,1)S(1)}, bf16[1536,1024]{1,0:T(8,128)(2,1)}, u32[]{:S(2)}) copy-start(bf16[1536,1024]{1,0:T(8,128)(2,1)} %get-tuple-element.866) | copy-start | bytes 9437188 | tf_op jit(solution)/shard_map/while
  87.8 8.6 %copy-start.10 = (bf16[128,768]{1,0:T(8,128)(2,1)S(1)}, bf16[128,768]{1,0:T(8,128)(2,1)}, u32[]{:S(2)}) copy-start(bf16[128,768]{1,0:T(8,128)(2,1)} %get-tuple-element.656) | copy-start | bytes 589828 | tf_op jit(solution)/shard_map/while
  87.8 8.6 %copy-start.12 = (bf16[128,736]{1,0:T(8,128)(2,1)S(1)}, bf16[128,736]{1,0:T(8,128)(2,1)}, u32[]{:S(2)}) copy-start(bf16[128,736]{1,0:T(8,128)(2,1)} %get-tuple-element.655) | copy-start | bytes 565252 | tf_op jit(solution)/shard_map/while
  87.8 10.0 %copy-start.6 = (bf16[128,704]{1,0:T(8,128)(2,1)S(1)}, bf16[128,704]{1,0:T(8,128)(2,1)}, u32[]{:S(2)}) copy-start(bf16[128,704]{1,0:T(8,128)(2,1)} %get-tuple-element.660) | copy-start | bytes 540676 | tf_op jit(solution)/shard_map/while
  87.8 10.0 %copy-start.8 = (bf16[128,672]{1,0:T(8,128)(2,1)S(1)}, bf16[128,672]{1,0:T(8,128)(2,1)}, u32[]{:S(2)}) copy-start(bf16[128,672]{1,0:T(8,128)(2,1)} %get-tuple-element.659) | copy-start | bytes 516100 | tf_op jit(solution)/shard_map/while
  87.8 11.5 %copy-start.18 = (bf16[128,640]{1,0:T(8,128)(2,1)S(1)}, bf16[128,640]{1,0:T(8,128)(2,1)}, u32[]{:S(2)}) copy-start(bf16[128,640]{1,0:T(8,128)(2,1)} %get-tuple-element.664) | copy-start | bytes 491524 | tf_op jit(solution)/shard_map/while
  87.8 11.5 %copy-start.20 = (bf16[128,608]{1,0:T(8,128)(2,1)S(1)}, bf16[128,608]{1,0:T(8,128)(2,1)}, u32[]{:S(2)}) copy-start(bf16[128,608]{1,0:T(8,128)(2,1)} %get-tuple-element.663) | copy-start | bytes 466948 | tf_op jit(solution)/shard_map/while
  88.1 12.7 %copy-start.14 = (bf16[128,576]{1,0:T(8,128)(2,1)S(1)}, bf16[128,576]{1,0:T(8,128)(2,1)}, u32[]{:S(2)}) copy-start(bf16[128,576]{1,0:T(8,128)(2,1)} %get-tuple-element.668) | copy-start | bytes 442372 | tf_op jit(solution)/shard_map/while
  88.1 12.6 %copy-start.16 = (bf16[128,544]{1,0:T(8,128)(2,1)S(1)}, bf16[128,544]{1,0:T(8,128)(2,1)}, u32[]{:S(2)}) copy-start(bf16[128,544]{1,0:T(8,128)(2,1)} %get-tuple-element.667) | copy-start | bytes 417796 | tf_op jit(solution)/shard_map/while
  107.0 13.0 %copy-start = (bf16[1536,1024]{1,0:T(8,128)(2,1)S(1)}, bf16[1536,1024]{1,0:T(8,128)(2,1)}, u32[]{:S(2)}) copy-start(bf16[1536,1024]{1,0:T(8,128)(2,1)} %get-tuple-element.866) | copy-start | bytes 9437188 | tf_op jit(solution)/shard_map/while
  137.7 8.6 %copy-start.10 = (bf16[128,768]{1,0:T(8,128)(2,1)S(1)}, bf16[128,768]{1,0:T(8,128)(2,1)}, u32[]{:S(2)}) copy-start(bf16[128,768]{1,0:T(8,128)(2,1)} %get-tuple-element.656) | copy-start | bytes 589828 | tf_op jit(solution)/shard_map/while
  137.7 8.6 %copy-start.12 = (bf16[128,736]{1,0:T(8,128)(2,1)S(1)}, bf16[128,736]{1,0:T(8,128)(2,1)}, u32[]{:S(2)}) copy-start(bf16[128,736]{1,0:T(8,128)(2,1)} %get-tuple-element.655) | copy-start | bytes 565252 | tf_op jit(solution)/shard_map/while
  137.7 10.0 %copy-start.6 = (bf16[128,704]{1,0:T(8,128)(2,1)S(1)}, bf16[128,704]{1,0:T(8,128)(2,1)}, u32[]{:S(2)}) copy-start(bf16[128,704]{1,0:T(8,128)(2,1)} %get-tuple-element.660) | copy-start | bytes 540676 | tf_op jit(solution)/shard_map/while
  137.7 10.0 %copy-start.8 = (bf16[128,672]{1,0:T(8,128)(2,1)S(1)}, bf16[128,672]{1,0:T(8,128)(2,1)}, u32[]{:S(2)}) copy-start(bf16[128,672]{1,0:T(8,128)(2,1)} %get-tuple-element.659) | copy-start | bytes 516100 | tf_op jit(solution)/shard_map/while
  137.7 11.5 %copy-start.18 = (bf16[128,640]{1,0:T(8,128)(2,1)S(1)}, bf16[128,640]{1,0:T(8,128)(2,1)}, u32[]{:S(2)}) copy-start(bf16[128,640]{1,0:T(8,128)(2,1)} %get-tuple-element.664) | copy-start | bytes 491524 | tf_op jit(solution)/shard_map/while
  137.8 11.5 %copy-start.20 = (bf16[128,608]{1,0:T(8,128)(2,1)S(1)}, bf16[128,608]{1,0:T(8,128)(2,1)}, u32[]{:S(2)}) copy-start(bf16[128,608]{1,0:T(8,128)(2,1)} %get-tuple-element.663) | copy-start | bytes 466948 | tf_op jit(solution)/shard_map/while
  138.1 12.7 %copy-start.14 = (bf16[128,576]{1,0:T(8,128)(2,1)S(1)}, bf16[128,576]{1,0:T(8,128)(2,1)}, u32[]{:S(2)}) copy-start(bf16[128,576]{1,0:T(8,128)(2,1)} %get-tuple-element.668) | copy-start | bytes 442372 | tf_op jit(solution)/shard_map/while
  138.1 12.6 %copy-start.16 = (bf16[128,544]{1,0:T(8,128)(2,1)S(1)}, bf16[128,544]{1,0:T(8,128)(2,1)}, u32[]{:S(2)}) copy-start(bf16[128,544]{1,0:T(8,128)(2,1)} %get-tuple-element.667) | copy-start | bytes 417796 | tf_op jit(solution)/shard_map/while
  156.9 13.0 %copy-start = (bf16[1536,1024]{1,0:T(8,128)(2,1)S(1)}, bf16[1536,1024]{1,0:T(8,128)(2,1)}, u32[]{:S(2)}) copy-start(bf16[1536,1024]{1,0:T(8,128)(2,1)} %get-tuple-element.866) | copy-start | bytes 9437188 | tf_op jit(solution)/shard_map/while
  187.6 8.6 %copy-start.10 = (bf16[128,768]{1,0:T(8,128)(2,1)S(1)}, bf16[128,768]{1,0:T(8,128)(2,1)}, u32[]{:S(2)}) copy-start(bf16[128,768]{1,0:T(8,128)(2,1)} %get-tuple-element.656) | copy-start | bytes 589828 | tf_op jit(solution)/shard_map/while
  187.6 8.6 %copy-start.12 = (bf16[128,736]{1,0:T(8,128)(2,1)S(1)}, bf16[128,736]{1,0:T(8,128)(2,1)}, u32[]{:S(2)}) copy-start(bf16[128,736]{1,0:T(8,128)(2,1)} %get-tuple-element.655) | copy-start | bytes 565252 | tf_op jit(solution)/shard_map/while
  187.6 10.0 %copy-start.6 = (bf16[128,704]{1,0:T(8,128)(2,1)S(1)}, bf16[128,704]{1,0:T(8,128)(2,1)}, u32[]{:S(2)}) copy-start(bf16[128,704]{1,0:T(8,128)(2,1)} %get-tuple-element.660) | copy-start | bytes 540676 | tf_op jit(solution)/shard_map/while
  187.6 10.0 %copy-start.8 = (bf16[128,672]{1,0:T(8,128)(2,1)S(1)}, bf16[128,672]{1,0:T(8,128)(2,1)}, u32[]{:S(2)}) copy-start(bf16[128,672]{1,0:T(8,128)(2,1)} %get-tuple-element.659) | copy-start | bytes 516100 | tf_op jit(solution)/shard_map/while
  187.7 11.5 %copy-start.18 = (bf16[128,640]{1,0:T(8,128)(2,1)S(1)}, bf16[128,640]{1,0:T(8,128)(2,1)}, u32[]{:S(2)}) copy-start(bf16[128,640]{1,0:T(8,128)(2,1)} %get-tuple-element.664) | copy-start | bytes 491524 | tf_op jit(solution)/shard_map/while
  187.7 11.5 %copy-start.20 = (bf16[128,608]{1,0:T(8,128)(2,1)S(1)}, bf16[128,608]{1,0:T(8,128)(2,1)}, u32[]{:S(2)}) copy-start(bf16[128,608]{1,0:T(8,128)(2,1)} %get-tuple-element.663) | copy-start | bytes 466948 | tf_op jit(solution)/shard_map/while
  188.0 12.7 %copy-start.14 = (bf16[128,576]{1,0:T(8,128)(2,1)S(1)}, bf16[128,576]{1,0:T(8,128)(2,1)}, u32[]{:S(2)}) copy-start(bf16[128,576]{1,0:T(8,128)(2,1)} %get-tuple-element.668) | copy-start | bytes 442372 | tf_op jit(solution)/shard_map/while
  188.0 12.6 %copy-start.16 = (bf16[128,544]{1,0:T(8,128)(2,1)S(1)}, bf16[128,544]{1,0:T(8,128)(2,1)}, u32[]{:S(2)}) copy-start(bf16[128,544]{1,0:T(8,128)(2,1)} %get-tuple-element.667) | copy-start | bytes 417796 | tf_op jit(solution)/shard_map/while
  206.8 13.0 %copy-start = (bf16[1536,1024]{1,0:T(8,128)(2,1)S(1)}, bf16[1536,1024]{1,0:T(8,128)(2,1)}, u32[]{:S(2)}) copy-start(bf16[1536,1024]{1,0:T(8,128)(2,1)} %get-tuple-element.866) | copy-start | bytes 9437188 | tf_op jit(solution)/shard_map/while
  237.5 8.6 %copy-start.12 = (bf16[128,736]{1,0:T(8,128)(2,1)S(1)}, bf16[128,736]{1,0:T(8,128)(2,1)}, u32[]{:S(2)}) copy-start(bf16[128,736]{1,0:T(8,128)(2,1)} %get-tuple-element.655) | copy-start | bytes 565252 | tf_op jit(solution)/shard_map/while
  237.5 10.0 %copy-start.6 = (bf16[128,704]{1,0:T(8,128)(2,1)S(1)}, bf16[128,704]{1,0:T(8,128)(2,1)}, u32[]{:S(2)}) copy-start(bf16[128,704]{1,0:T(8,128)(2,1)} %get-tuple-element.660) | copy-start | bytes 540676 | tf_op jit(solution)/shard_map/while
  237.6 10.0 %copy-start.8 = (bf16[128,672]{1,0:T(8,128)(2,1)S(1)}, bf16[128,672]{1,0:T(8,128)(2,1)}, u32[]{:S(2)}) copy-start(bf16[128,672]{1,0:T(8,128)(2,1)} %get-tuple-element.659) | copy-start | bytes 516100 | tf_op jit(solution)/shard_map/while
  237.6 11.5 %copy-start.18 = (bf16[128,640]{1,0:T(8,128)(2,1)S(1)}, bf16[128,640]{1,0:T(8,128)(2,1)}, u32[]{:S(2)}) copy-start(bf16[128,640]{1,0:T(8,128)(2,1)} %get-tuple-element.664) | copy-start | bytes 491524 | tf_op jit(solution)/shard_map/while
  237.6 11.5 %copy-start.20 = (bf16[128,608]{1,0:T(8,128)(2,1)S(1)}, bf16[128,608]{1,0:T(8,128)(2,1)}, u32[]{:S(2)}) copy-start(bf16[128,608]{1,0:T(8,128)(2,1)} %get-tuple-element.663) | copy-start | bytes 466948 | tf_op jit(solution)/shard_map/while
  237.9 12.7 %copy-start.14 = (bf16[128,576]{1,0:T(8,128)(2,1)S(1)}, bf16[128,576]{1,0:T(8,128)(2,1)}, u32[]{:S(2)}) copy-start(bf16[128,576]{1,0:T(8,128)(2,1)} %get-tuple-element.668) | copy-start | bytes 442372 | tf_op jit(solution)/shard_map/while
  237.9 12.6 %copy-start.16 = (bf16[128,544]{1,0:T(8,128)(2,1)S(1)}, bf16[128,544]{1,0:T(8,128)(2,1)}, u32[]{:S(2)}) copy-start(bf16[128,544]{1,0:T(8,128)(2,1)} %get-tuple-element.667) | copy-start | bytes 417796 | tf_op jit(solution)/shard_map/while
  276.6 48.1 %copy-start.1 = (bf16[1536,1024]{1,0:T(8,128)(2,1)S(1)}, bf16[1536,1024]{1,0:T(8,128)(2,1)}, u32[]{:S(2)}) copy-start(bf16[1536,1024]{1,0:T(8,128)(2,1)} %get-tuple-element.1109) | copy-start | bytes 9437188
  351.4 10.0 %copy-start.7 = (bf16[128,704]{1,0:T(8,128)(2,1)S(1)}, bf16[128,704]{1,0:T(8,128)(2,1)}, u32[]{:S(2)}) copy-start(bf16[128,704]{1,0:T(8,128)(2,1)} %get-tuple-element.729) | copy-start | bytes 540676 | tf_op jit(solution)/shard_map/while
  351.4 10.0 %copy-start.9 = (bf16[128,672]{1,0:T(8,128)(2,1)S(1)}, bf16[128,672]{1,0:T(8,128)(2,1)}, u32[]{:S(2)}) copy-start(bf16[128,672]{1,0:T(8,128)(2,1)} %get-tuple-element.728) | copy-start | bytes 516100 | tf_op jit(solution)/shard_map/while
  351.4 11.5 %copy-start.19 = (bf16[128,640]{1,0:T(8,128)(2,1)S(1)}, bf16[128,640]{1,0:T(8,128)(2,1)}, u32[]{:S(2)}) copy-start(bf16[128,640]{1,0:T(8,128)(2,1)} %get-tuple-element.733) | copy-start | bytes 491524 | tf_op jit(solution)/shard_map/while
  351.4 11.5 %copy-start.21 = (bf16[128,608]{1,0:T(8,128)(2,1)S(1)}, bf16[128,608]{1,0:T(8,128)(2,1)}, u32[]{:S(2)}) copy-start(bf16[128,608]{1,0:T(8,128)(2,1)} %get-tuple-element.732) | copy-start | bytes 466948 | tf_op jit(solution)/shard_map/while
  351.7 12.6 %copy-start.15 = (bf16[128,576]{1,0:T(8,128)(2,1)S(1)}, bf16[128,576]{1,0:T(8,128)(2,1)}, u32[]{:S(2)}) copy-start(bf16[128,576]{1,0:T(8,128)(2,1)} %get-tuple-element.737) | copy-start | bytes 442372 | tf_op jit(solution)/shard_map/while
  351.7 12.6 %copy-start.17 = (bf16[128,544]{1,0:T(8,128)(2,1)S(1)}, bf16[128,544]{1,0:T(8,128)(2,1)}, u32[]{:S(2)}) copy-start(bf16[128,544]{1,0:T(8,128)(2,1)} %get-tuple-element.736) | copy-start | bytes 417796 | tf_op jit(solution)/shard_map/while
  397.2 10.0 %copy-start.7 = (bf16[128,704]{1,0:T(8,128)(2,1)S(1)}, bf16[128,704]{1,0:T(8,128)(2,1)}, u32[]{:S(2)}) copy-start(bf16[128,704]{1,0:T(8,128)(2,1)} %get-tuple-element.729) | copy-start | bytes 540676 | tf_op jit(solution)/shard_map/while
  397.2 10.0 %copy-start.9 = (bf16[128,672]{1,0:T(8,128)(2,1)S(1)}, bf16[128,672]{1,0:T(8,128)(2,1)}, u32[]{:S(2)}) copy-start(bf16[128,672]{1,0:T(8,128)(2,1)} %get-tuple-element.728) | copy-start | bytes 516100 | tf_op jit(solution)/shard_map/while
  397.2 11.5 %copy-start.19 = (bf16[128,640]{1,0:T(8,128)(2,1)S(1)}, bf16[128,640]{1,0:T(8,128)(2,1)}, u32[]{:S(2)}) copy-start(bf16[128,640]{1,0:T(8,128)(2,1)} %get-tuple-element.733) | copy-start | bytes 491524 | tf_op jit(solution)/shard_map/while
  397.2 11.5 %copy-start.21 = (bf16[128,608]{1,0:T(8,128)(2,1)S(1)}, bf16[128,608]{1,0:T(8,128)(2,1)}, u32[]{:S(2)}) copy-start(bf16[128,608]{1,0:T(8,128)(2,1)} %get-tuple-element.732) | copy-start | bytes 466948 | tf_op jit(solution)/shard_map/while
  397.6 12.6 %copy-start.15 = (bf16[128,576]{1,0:T(8,128)(2,1)S(1)}, bf16[128,576]{1,0:T(8,128)(2,1)}, u32[]{:S(2)}) copy-start(bf16[128,576]{1,0:T(8,128)(2,1)} %get-tuple-element.737) | copy-start | bytes 442372 | tf_op jit(solution)/shard_map/while
  397.6 12.6 %copy-start.17 = (bf16[128,544]{1,0:T(8,128)(2,1)S(1)}, bf16[128,544]{1,0:T(8,128)(2,1)}, u32[]{:S(2)}) copy-start(bf16[128,544]{1,0:T(8,128)(2,1)} %get-tuple-element.736) | copy-start | bytes 417796 | tf_op jit(solution)/shard_map/while
  443.0 10.0 %copy-start.7 = (bf16[128,704]{1,0:T(8,128)(2,1)S(1)}, bf16[128,704]{1,0:T(8,128)(2,1)}, u32[]{:S(2)}) copy-start(bf16[128,704]{1,0:T(8,128)(2,1)} %get-tuple-element.729) | copy-start | bytes 540676 | tf_op jit(solution)/shard_map/while
  443.0 10.0 %copy-start.9 = (bf16[128,672]{1,0:T(8,128)(2,1)S(1)}, bf16[128,672]{1,0:T(8,128)(2,1)}, u32[]{:S(2)}) copy-start(bf16[128,672]{1,0:T(8,128)(2,1)} %get-tuple-element.728) | copy-start | bytes 516100 | tf_op jit(solution)/shard_map/while
  443.1 11.5 %copy-start.19 = (bf16[128,640]{1,0:T(8,128)(2,1)S(1)}, bf16[128,640]{1,0:T(8,128)(2,1)}, u32[]{:S(2)}) copy-start(bf16[128,640]{1,0:T(8,128)(2,1)} %get-tuple-element.733) | copy-start | bytes 491524 | tf_op jit(solution)/shard_map/while
  443.1 11.5 %copy-start.21 = (bf16[128,608]{1,0:T(8,128)(2,1)S(1)}, bf16[128,608]{1,0:T(8,128)(2,1)}, u32[]{:S(2)}) copy-start(bf16[128,608]{1,0:T(8,128)(2,1)} %get-tuple-element.732) | copy-start | bytes 466948 | tf_op jit(solution)/shard_map/while
  443.4 12.6 %copy-start.15 = (bf16[128,576]{1,0:T(8,128)(2,1)S(1)}, bf16[128,576]{1,0:T(8,128)(2,1)}, u32[]{:S(2)}) copy-start(bf16[128,576]{1,0:T(8,128)(2,1)} %get-tuple-element.737) | copy-start | bytes 442372 | tf_op jit(solution)/shard_map/while
  443.4 12.6 %copy-start.17 = (bf16[128,544]{1,0:T(8,128)(2,1)S(1)}, bf16[128,544]{1,0:T(8,128)(2,1)}, u32[]{:S(2)}) copy-start(bf16[128,544]{1,0:T(8,128)(2,1)} %get-tuple-element.736) | copy-start | bytes 417796 | tf_op jit(solution)/shard_map/while
  488.8 10.0 %copy-start.7 = (bf16[128,704]{1,0:T(8,128)(2,1)S(1)}, bf16[128,704]{1,0:T(8,128)(2,1)}, u32[]{:S(2)}) copy-start(bf16[128,704]{1,0:T(8,128)(2,1)} %get-tuple-element.729) | copy-start | bytes 540676 | tf_op jit(solution)/shard_map/while
  488.9 10.0 %copy-start.9 = (bf16[128,672]{1,0:T(8,128)(2,1)S(1)}, bf16[128,672]{1,0:T(8,128)(2,1)}, u32[]{:S(2)}) copy-start(bf16[128,672]{1,0:T(8,128)(2,1)} %get-tuple-element.728) | copy-start | bytes 516100 | tf_op jit(solution)/shard_map/while
  488.9 11.5 %copy-start.19 = (bf16[128,640]{1,0:T(8,128)(2,1)S(1)}, bf16[128,640]{1,0:T(8,128)(2,1)}, u32[]{:S(2)}) copy-start(bf16[128,640]{1,0:T(8,128)(2,1)} %get-tuple-element.733) | copy-start | bytes 491524 | tf_op jit(solution)/shard_map/while
  488.9 11.5 %copy-start.21 = (bf16[128,608]{1,0:T(8,128)(2,1)S(1)}, bf16[128,608]{1,0:T(8,128)(2,1)}, u32[]{:S(2)}) copy-start(bf16[128,608]{1,0:T(8,128)(2,1)} %get-tuple-element.732) | copy-start | bytes 466948 | tf_op jit(solution)/shard_map/while
  489.2 12.6 %copy-start.15 = (bf16[128,576]{1,0:T(8,128)(2,1)S(1)}, bf16[128,576]{1,0:T(8,128)(2,1)}, u32[]{:S(2)}) copy-start(bf16[128,576]{1,0:T(8,128)(2,1)} %get-tuple-element.737) | copy-start | bytes 442372 | tf_op jit(solution)/shard_map/while
  489.2 12.6 %copy-start.17 = (bf16[128,544]{1,0:T(8,128)(2,1)S(1)}, bf16[128,544]{1,0:T(8,128)(2,1)}, u32[]{:S(2)}) copy-start(bf16[128,544]{1,0:T(8,128)(2,1)} %get-tuple-element.736) | copy-start | bytes 417796 | tf_op jit(solution)/shard_map/while
  (27 other events, 201.9 us)
Sparse Core Ops, SparseCore 0:
  39.3 14.3 all-gather.2
  259.4 10.2 all-gather.4
where the time goes:
time: 520 us; the launch traced here: 518 us
  local copies, waits for them, and re-layouts  381 us (73%)
  blocking collectives  34.8 us (7%)
  matrix products  23.9 us (5%)
  waiting for transfers between devices  22.9 us (4%)
  other arithmetic  21.4 us (4%)
  between operations  14.2 us (3%)
  loops' own time  13.2 us (3%)
  starting transfers between devices  6.27 us (1%)
    while x416, local copies, waits for them, and re-layouts  178 us
    slice x120, local copies, waits for them, and re-layouts, shift_slots(): segment[:, :segment.shape[1] - moved * BLK]  98.7 us
    dynamic_slice x136, local copies, waits for them, and re-layouts, one_group(): lax.dynamic_slice_in_dim(segment, first_slot * BLK, column_slots * BLK, 1)  45.4 us
    psum x1, blocking collectives, per_device(): total_squared = lax.psum(trace_squared, ('row', 'col'))  34.8 us
    dot_general x8, matrix products, one_group(): jnp.einsum('gak,gkn->gan', left_rows, gathered, preferred_element_type=jn...  23.9 us
    ppermute x1, waiting for transfers between devices, extended_2(): before = lax.ppermute(last, axis, up)  21.1 us
    another operation x2, loops' own time, band_part(): lax.map(one_group, jnp.arange(block_rows // group_rows, dtype=jnp.int32))  13.2 us
    transpose x2, other arithmetic, diagonal_sum(): jnp.diagonal(values.reshape(block_rows, BLK, slot_total, BLK), axis1=1, a...  11.4 us
  transfers between devices with their start and end apart: 4, of which 2 were waited for; matrix products, arithmetic and copies ran while one was open for 8% of the time, Pallas kernels for 0%

commit v1 on v0

--- a/solution.py
+++ b/solution.py
@@ -140,7 +140,7 @@
         collect_half,
     )
     trace_squared = diagonal_sum(squared, chosen)
-    total_squared = lax.psum(trace_squared, ("row", "col"))
+    total_squared = jnp.sum(lax.all_gather(trace_squared, ("row", "col")), axis=0)
     order_total = block_total * BLK
     traces = jnp.stack([total_kept, total_squared]) / order_total
     return (purified, traces)

time: 520 us -> 522 us (level)
    psum x1 -> x0, blocking collectives: 34.8 us -> none  [per_device(): total_squared = lax.psum(trace_squared, ('row', 'col'))]
    unnamed x0 -> x1, blocking collectives: none -> 34.8 us
  transfers between devices with their start and end apart: 4 -> 4, of which waited for: 2 -> 2; matrix products, arithmetic and copies ran while one was open for 8% -> 9% of each run, Pallas kernels for 0% -> 0%
where the time goes in v1:
time: 522 us; the launch traced here: 520 us
  local copies, waits for them, and re-layouts  383 us (73%)
  blocking collectives  34.8 us (7%)
  matrix products  23.9 us (5%)
  waiting for transfers between devices  22.9 us (4%)
  other arithmetic  22.1 us (4%)
  between operations  14.2 us (3%)
  loops' own time  12.7 us (2%)
  starting transfers between devices  6.27 us (1%)
    while x416, local copies, waits for them, and re-layouts  178 us
    slice x120, local copies, waits for them, and re-layouts, shift_slots(): segment[:, :segment.shape[1] - moved * BLK]  98.8 us
    dynamic_slice x136, local copies, waits for them, and re-layouts, one_group(): lax.dynamic_slice_in_dim(segment, first_slot * BLK, column_slots * BLK, 1)  45.4 us
    unnamed x1, blocking collectives  34.8 us
    dot_general x8, matrix products, one_group(): jnp.einsum('gak,gkn->gan', left_rows, gathered, preferred_element_type=jn...  23.9 us
    ppermute x1, waiting for transfers between devices, extended_2(): before = lax.ppermute(last, axis, up)  21.1 us
    another operation x2, loops' own time, band_part(): lax.map(one_group, jnp.arange(block_rows // group_rows, dtype=jnp.int32))  12.7 us
    transpose x2, other arithmetic, diagonal_sum(): jnp.diagonal(values.reshape(block_rows, BLK, slot_total, BLK), axis1=1, a...  11.4 us
  transfers between devices with their start and end apart: 4, of which 2 were waited for; matrix products, arithmetic and copies ran while one was open for 9% of the time, Pallas kernels for 0%

profile of v1, /device:TPU:0, one launch (start us, length us, event | category | flops | bytes accessed | tf_op | source)
XLA Modules:
  0.0 519.9 jit_solution(238078020381052510)
XLA Ops:
  8.4 2.1 mul.804
  10.6 4.9 collective-permute-start
  15.5 1.3 collective-permute-start.1
  16.8 21.1 %collective-permute-done = bf16[512,512]{1,0:T(8,128)(2,1)S(1)} collective-permute-done((bf16[512,512]{1,0:T(8,128)(2,1)S(1)}, bf16[512,512]{1,0:T(8,128)(2,1)S(1)}, u32[]{:S(2)}, u32[]{:S(2)}) %collective-permute-start) | collective-permute-done | bytes 524320 | tf_op jit(solution)/shard_map/ppermute | solution.py:16
  37.9 1.2 pad_maximum_fusion
  39.2 1.2 reshape.769
  40.5 4.3 copy.7
  44.8 2.4 mul.808.clone
  47.2 4.7 mul.809
  51.9 1.8 all-gather.3.cloned.1.call-done
  53.7 2.3 slice.442
  57.1 199.6 %while.26 = (s32[]{:T(128)}, f32[4,128,512]{2,1,0:T(8,128)}, s32[4]{0:T(128)S(1)}, bf16[512,1024]{1,0:T(8,128)(2,1)}, bf16[1536,1024]{1,0:T(8,128)(2,1)}, /*inde...) while((s32[]{:T(128)}, f32[4,128,512]{2,1,0:T(8,128)}, ...), condition=%wide.region_1.2_spmd, body=%wide.region_0.1_spmd.sunk | while | flops 134217904 | bytes 56200764 | solution.py:83
  58.7 1.7 constant_dynamic-slice_fusion.65
  60.4 1.7 constant_dynamic-slice_fusion.66
  63.5 1.1 fusion.26
  65.3 1.6 constant_dynamic-update-slice_fusion.129
  66.9 1.6 constant_dynamic-update-slice_fusion.130
  68.4 1.7 constant_dynamic-slice_fusion.67
  103.2 3.0 fusion.27
  108.6 1.7 constant_dynamic-slice_fusion.65
  110.3 1.7 constant_dynamic-slice_fusion.66
  113.4 1.1 fusion.26
  115.2 1.6 constant_dynamic-update-slice_fusion.129
  116.8 1.6 constant_dynamic-update-slice_fusion.130
  118.3 1.7 constant_dynamic-slice_fusion.67
  153.1 3.0 fusion.27
  158.5 1.7 constant_dynamic-slice_fusion.65
  160.2 1.7 constant_dynamic-slice_fusion.66
  163.3 1.1 fusion.26
  165.1 1.6 constant_dynamic-update-slice_fusion.129
  166.7 1.6 constant_dynamic-update-slice_fusion.130
  168.3 1.7 constant_dynamic-slice_fusion.67
  203.1 3.0 fusion.27
  208.4 1.7 constant_dynamic-slice_fusion.65
  210.1 1.7 constant_dynamic-slice_fusion.66
  213.2 1.1 fusion.26
  215.0 1.6 constant_dynamic-update-slice_fusion.129
  216.6 1.6 constant_dynamic-update-slice_fusion.130
  218.1 1.7 constant_dynamic-slice_fusion.67
  252.9 3.0 fusion.27
  256.7 2.5 fusion.4
  259.2 4.6 multiply_bitcast_fusion
  263.8 2.8 gather_fusion
  267.3 2.7 reshape_reshape.10
  269.9 7.3 %copy.8 = f32[16,32,16,32]{2,0,3,1:T(8,128)} copy(f32[16,32,16,32]{3,2,1,0:T(8,128)} %reshape_reshape.10) | data formatting | bytes 2097152 | tf_op jit(solution)/shard_map/reshape;reshape | solution.py:32
  277.2 6.8 %fusion = bf16[16,16,32,32]{1,0,3,2:T(8,128)(2,1)} fusion(f32[16,32,16,32]{2,0,3,1:T(8,128)} %copy.8, f32[16,16]{1,0:T(8,128)S(1)} %get-tuple-element.403), kind=kLoop, calls=%fused_computation.163 | loop fusion | flops 524288 | bytes 1573888 | tf_op jit(solution)/shard_map/jit(diagonal)/transpose | solution.py:90
  284.0 2.8 gather_fusion.1
  287.6 1.3 dynamic-update-slice
  288.9 34.8 %all-reduce.63 = (f32[16]{0:T(128)S(1)}, f32[1]{0:T(128)}) all-reduce(f32[16]{0:T(128)S(1)} %dynamic-update-slice, f32[1]{0:T(128)} %bitcast.138), channel_id=1, replica_groups=mesh['snap'=2,'row'=8,'col'=2] {'row','col'}, use_global_device_ids=true, to_apply=%add.62 | all-reduce | flops 17 | bytes 136
  324.4 1.8 maximum_multiply_fusion
  327.3 183.0 %while.27 = (s32[]{:T(128)}, f32[4,128,512]{2,1,0:T(8,128)}, s32[4]{0:T(128)S(1)}, bf16[512,1024]{1,0:T(8,128)(2,1)}, bf16[1536,1024]{1,0:T(8,128)(2,1)S(1)}, /*...) while((s32[]{:T(128)}, f32[4,128,512]{2,1,0:T(8,128)}, ...), condition=%wide.region_3.4_spmd, body=%wide.region_2.3_spmd.sunk | while | flops 134217904 | bytes 43617860 | solution.py:83
  332.3 1.6 constant_dynamic-update-slice_fusion.161
  333.9 1.6 constant_dynamic-update-slice_fusion.162
  369.3 3.0 fusion.31
  378.1 1.6 constant_dynamic-update-slice_fusion.161
  379.6 1.6 constant_dynamic-update-slice_fusion.162
  415.1 3.0 fusion.31
  423.8 1.6 constant_dynamic-update-slice_fusion.161
  425.4 1.6 constant_dynamic-update-slice_fusion.162
  460.8 3.0 fusion.31
  469.5 1.6 constant_dynamic-update-slice_fusion.161
  471.1 1.6 constant_dynamic-update-slice_fusion.162
  506.6 3.0 fusion.31
  510.3 2.8 fusion.3
  (700 shorter events, 301.6 us)
Async XLA Ops:
  7.2 46.5 %all-gather.3.cloned.1.call-start = ((), (), s32[]{:S(2)}) async-start(), calls=%async_computation | async-start | bytes 4718592 | tf_op jit(solution)/shard_map/all_gather | solution.py:126
  10.6 27.3 %collective-permute-start = (bf16[512,512]{1,0:T(8,128)(2,1)S(1)}, bf16[512,512]{1,0:T(8,128)(2,1)S(1)}, u32[]{:S(2)}, u32[]{:S(2)}) collective-permute-start(bf16[512,512]{1,0:T(8,128)(2,1)S(1)} %mul.805), channel_id=1, source_target_pairs={{0,2},{2,4},{4,6},{6,8},{8,10},{10,12},{12,14},{1,3},{3,5},{5,7},{... | collective-permute-start | bytes 1572872 | tf_op jit(solution)/shard_map/ppermute | solution.py:16
  15.5 22.4 %collective-permute-start.1 = (bf16[512,512]{1,0:T(8,128)(2,1)S(1)}, bf16[512,512]{1,0:T(8,128)(2,1)S(1)}, u32[]{:S(2)}, u32[]{:S(2)}) collective-permute-start(bf16[512,512]{1,0:T(8,128)(2,1)S(1)} %mul.805), channel_id=1, source_target_pairs={{2,0},{4,2},{6,4},{8,6},{10,8},{12,10},{14,12},{3,1},{5,3},{7,5},{... | collective-permute-start | bytes 1572872 | tf_op jit(solution)/shard_map/ppermute | solution.py:17
  39.2 287.0 %all-gather.5.cloned.1.call-start = ((), (), s32[]{:S(2)}) async-start(), calls=%async_computation.1 | async-start | bytes 1572864 | tf_op jit(solution)/shard_map/all_gather | solution.py:130
  57.1 13.1 %copy-start = (bf16[1536,1024]{1,0:T(8,128)(2,1)S(1)}, bf16[1536,1024]{1,0:T(8,128)(2,1)}, u32[]{:S(2)}) copy-start(bf16[1536,1024]{1,0:T(8,128)(2,1)} %get-tuple-element.866) | copy-start | bytes 9437188 | tf_op jit(solution)/shard_map/while
  87.8 8.6 %copy-start.10 = (bf16[128,768]{1,0:T(8,128)(2,1)S(1)}, bf16[128,768]{1,0:T(8,128)(2,1)}, u32[]{:S(2)}) copy-start(bf16[128,768]{1,0:T(8,128)(2,1)} %get-tuple-element.656) | copy-start | bytes 589828 | tf_op jit(solution)/shard_map/while
  87.8 8.6 %copy-start.12 = (bf16[128,736]{1,0:T(8,128)(2,1)S(1)}, bf16[128,736]{1,0:T(8,128)(2,1)}, u32[]{:S(2)}) copy-start(bf16[128,736]{1,0:T(8,128)(2,1)} %get-tuple-element.655) | copy-start | bytes 565252 | tf_op jit(solution)/shard_map/while
  87.8 10.0 %copy-start.6 = (bf16[128,704]{1,0:T(8,128)(2,1)S(1)}, bf16[128,704]{1,0:T(8,128)(2,1)}, u32[]{:S(2)}) copy-start(bf16[128,704]{1,0:T(8,128)(2,1)} %get-tuple-element.660) | copy-start | bytes 540676 | tf_op jit(solution)/shard_map/while
  87.8 10.0 %copy-start.8 = (bf16[128,672]{1,0:T(8,128)(2,1)S(1)}, bf16[128,672]{1,0:T(8,128)(2,1)}, u32[]{:S(2)}) copy-start(bf16[128,672]{1,0:T(8,128)(2,1)} %get-tuple-element.659) | copy-start | bytes 516100 | tf_op jit(solution)/shard_map/while
  87.8 11.5 %copy-start.18 = (bf16[128,640]{1,0:T(8,128)(2,1)S(1)}, bf16[128,640]{1,0:T(8,128)(2,1)}, u32[]{:S(2)}) copy-start(bf16[128,640]{1,0:T(8,128)(2,1)} %get-tuple-element.664) | copy-start | bytes 491524 | tf_op jit(solution)/shard_map/while
  87.8 11.5 %copy-start.20 = (bf16[128,608]{1,0:T(8,128)(2,1)S(1)}, bf16[128,608]{1,0:T(8,128)(2,1)}, u32[]{:S(2)}) copy-start(bf16[128,608]{1,0:T(8,128)(2,1)} %get-tuple-element.663) | copy-start | bytes 466948 | tf_op jit(solution)/shard_map/while
  88.1 12.6 %copy-start.14 = (bf16[128,576]{1,0:T(8,128)(2,1)S(1)}, bf16[128,576]{1,0:T(8,128)(2,1)}, u32[]{:S(2)}) copy-start(bf16[128,576]{1,0:T(8,128)(2,1)} %get-tuple-element.668) | copy-start | bytes 442372 | tf_op jit(solution)/shard_map/while
  88.1 12.6 %copy-start.16 = (bf16[128,544]{1,0:T(8,128)(2,1)S(1)}, bf16[128,544]{1,0:T(8,128)(2,1)}, u32[]{:S(2)}) copy-start(bf16[128,544]{1,0:T(8,128)(2,1)} %get-tuple-element.667) | copy-start | bytes 417796 | tf_op jit(solution)/shard_map/while
  107.0 13.1 %copy-start = (bf16[1536,1024]{1,0:T(8,128)(2,1)S(1)}, bf16[1536,1024]{1,0:T(8,128)(2,1)}, u32[]{:S(2)}) copy-start(bf16[1536,1024]{1,0:T(8,128)(2,1)} %get-tuple-element.866) | copy-start | bytes 9437188 | tf_op jit(solution)/shard_map/while
  137.7 8.6 %copy-start.10 = (bf16[128,768]{1,0:T(8,128)(2,1)S(1)}, bf16[128,768]{1,0:T(8,128)(2,1)}, u32[]{:S(2)}) copy-start(bf16[128,768]{1,0:T(8,128)(2,1)} %get-tuple-element.656) | copy-start | bytes 589828 | tf_op jit(solution)/shard_map/while
  137.7 8.6 %copy-start.12 = (bf16[128,736]{1,0:T(8,128)(2,1)S(1)}, bf16[128,736]{1,0:T(8,128)(2,1)}, u32[]{:S(2)}) copy-start(bf16[128,736]{1,0:T(8,128)(2,1)} %get-tuple-element.655) | copy-start | bytes 565252 | tf_op jit(solution)/shard_map/while
  137.7 10.0 %copy-start.6 = (bf16[128,704]{1,0:T(8,128)(2,1)S(1)}, bf16[128,704]{1,0:T(8,128)(2,1)}, u32[]{:S(2)}) copy-start(bf16[128,704]{1,0:T(8,128)(2,1)} %get-tuple-element.660) | copy-start | bytes 540676 | tf_op jit(solution)/shard_map/while
  137.7 10.0 %copy-start.8 = (bf16[128,672]{1,0:T(8,128)(2,1)S(1)}, bf16[128,672]{1,0:T(8,128)(2,1)}, u32[]{:S(2)}) copy-start(bf16[128,672]{1,0:T(8,128)(2,1)} %get-tuple-element.659) | copy-start | bytes 516100 | tf_op jit(solution)/shard_map/while
  137.7 11.5 %copy-start.18 = (bf16[128,640]{1,0:T(8,128)(2,1)S(1)}, bf16[128,640]{1,0:T(8,128)(2,1)}, u32[]{:S(2)}) copy-start(bf16[128,640]{1,0:T(8,128)(2,1)} %get-tuple-element.664) | copy-start | bytes 491524 | tf_op jit(solution)/shard_map/while
  137.7 11.5 %copy-start.20 = (bf16[128,608]{1,0:T(8,128)(2,1)S(1)}, bf16[128,608]{1,0:T(8,128)(2,1)}, u32[]{:S(2)}) copy-start(bf16[128,608]{1,0:T(8,128)(2,1)} %get-tuple-element.663) | copy-start | bytes 466948 | tf_op jit(solution)/shard_map/while
  138.0 12.6 %copy-start.14 = (bf16[128,576]{1,0:T(8,128)(2,1)S(1)}, bf16[128,576]{1,0:T(8,128)(2,1)}, u32[]{:S(2)}) copy-start(bf16[128,576]{1,0:T(8,128)(2,1)} %get-tuple-element.668) | copy-start | bytes 442372 | tf_op jit(solution)/shard_map/while
  138.0 12.6 %copy-start.16 = (bf16[128,544]{1,0:T(8,128)(2,1)S(1)}, bf16[128,544]{1,0:T(8,128)(2,1)}, u32[]{:S(2)}) copy-start(bf16[128,544]{1,0:T(8,128)(2,1)} %get-tuple-element.667) | copy-start | bytes 417796 | tf_op jit(solution)/shard_map/while
  156.9 13.1 %copy-start = (bf16[1536,1024]{1,0:T(8,128)(2,1)S(1)}, bf16[1536,1024]{1,0:T(8,128)(2,1)}, u32[]{:S(2)}) copy-start(bf16[1536,1024]{1,0:T(8,128)(2,1)} %get-tuple-element.866) | copy-start | bytes 9437188 | tf_op jit(solution)/shard_map/while
  187.6 8.6 %copy-start.10 = (bf16[128,768]{1,0:T(8,128)(2,1)S(1)}, bf16[128,768]{1,0:T(8,128)(2,1)}, u32[]{:S(2)}) copy-start(bf16[128,768]{1,0:T(8,128)(2,1)} %get-tuple-element.656) | copy-start | bytes 589828 | tf_op jit(solution)/shard_map/while
  187.6 8.6 %copy-start.12 = (bf16[128,736]{1,0:T(8,128)(2,1)S(1)}, bf16[128,736]{1,0:T(8,128)(2,1)}, u32[]{:S(2)}) copy-start(bf16[128,736]{1,0:T(8,128)(2,1)} %get-tuple-element.655) | copy-start | bytes 565252 | tf_op jit(solution)/shard_map/while
  187.6 10.0 %copy-start.6 = (bf16[128,704]{1,0:T(8,128)(2,1)S(1)}, bf16[128,704]{1,0:T(8,128)(2,1)}, u32[]{:S(2)}) copy-start(bf16[128,704]{1,0:T(8,128)(2,1)} %get-tuple-element.660) | copy-start | bytes 540676 | tf_op jit(solution)/shard_map/while
  187.6 10.0 %copy-start.8 = (bf16[128,672]{1,0:T(8,128)(2,1)S(1)}, bf16[128,672]{1,0:T(8,128)(2,1)}, u32[]{:S(2)}) copy-start(bf16[128,672]{1,0:T(8,128)(2,1)} %get-tuple-element.659) | copy-start | bytes 516100 | tf_op jit(solution)/shard_map/while
  187.6 11.5 %copy-start.18 = (bf16[128,640]{1,0:T(8,128)(2,1)S(1)}, bf16[128,640]{1,0:T(8,128)(2,1)}, u32[]{:S(2)}) copy-start(bf16[128,640]{1,0:T(8,128)(2,1)} %get-tuple-element.664) | copy-start | bytes 491524 | tf_op jit(solution)/shard_map/while
  187.6 11.5 %copy-start.20 = (bf16[128,608]{1,0:T(8,128)(2,1)S(1)}, bf16[128,608]{1,0:T(8,128)(2,1)}, u32[]{:S(2)}) copy-start(bf16[128,608]{1,0:T(8,128)(2,1)} %get-tuple-element.663) | copy-start | bytes 466948 | tf_op jit(solution)/shard_map/while
  187.9 12.6 %copy-start.14 = (bf16[128,576]{1,0:T(8,128)(2,1)S(1)}, bf16[128,576]{1,0:T(8,128)(2,1)}, u32[]{:S(2)}) copy-start(bf16[128,576]{1,0:T(8,128)(2,1)} %get-tuple-element.668) | copy-start | bytes 442372 | tf_op jit(solution)/shard_map/while
  187.9 12.6 %copy-start.16 = (bf16[128,544]{1,0:T(8,128)(2,1)S(1)}, bf16[128,544]{1,0:T(8,128)(2,1)}, u32[]{:S(2)}) copy-start(bf16[128,544]{1,0:T(8,128)(2,1)} %get-tuple-element.667) | copy-start | bytes 417796 | tf_op jit(solution)/shard_map/while
  206.8 13.1 %copy-start = (bf16[1536,1024]{1,0:T(8,128)(2,1)S(1)}, bf16[1536,1024]{1,0:T(8,128)(2,1)}, u32[]{:S(2)}) copy-start(bf16[1536,1024]{1,0:T(8,128)(2,1)} %get-tuple-element.866) | copy-start | bytes 9437188 | tf_op jit(solution)/shard_map/while
  237.5 8.6 %copy-start.12 = (bf16[128,736]{1,0:T(8,128)(2,1)S(1)}, bf16[128,736]{1,0:T(8,128)(2,1)}, u32[]{:S(2)}) copy-start(bf16[128,736]{1,0:T(8,128)(2,1)} %get-tuple-element.655) | copy-start | bytes 565252 | tf_op jit(solution)/shard_map/while
  237.5 10.0 %copy-start.6 = (bf16[128,704]{1,0:T(8,128)(2,1)S(1)}, bf16[128,704]{1,0:T(8,128)(2,1)}, u32[]{:S(2)}) copy-start(bf16[128,704]{1,0:T(8,128)(2,1)} %get-tuple-element.660) | copy-start | bytes 540676 | tf_op jit(solution)/shard_map/while
  237.5 10.0 %copy-start.8 = (bf16[128,672]{1,0:T(8,128)(2,1)S(1)}, bf16[128,672]{1,0:T(8,128)(2,1)}, u32[]{:S(2)}) copy-start(bf16[128,672]{1,0:T(8,128)(2,1)} %get-tuple-element.659) | copy-start | bytes 516100 | tf_op jit(solution)/shard_map/while
  237.5 11.5 %copy-start.18 = (bf16[128,640]{1,0:T(8,128)(2,1)S(1)}, bf16[128,640]{1,0:T(8,128)(2,1)}, u32[]{:S(2)}) copy-start(bf16[128,640]{1,0:T(8,128)(2,1)} %get-tuple-element.664) | copy-start | bytes 491524 | tf_op jit(solution)/shard_map/while
  237.5 11.5 %copy-start.20 = (bf16[128,608]{1,0:T(8,128)(2,1)S(1)}, bf16[128,608]{1,0:T(8,128)(2,1)}, u32[]{:S(2)}) copy-start(bf16[128,608]{1,0:T(8,128)(2,1)} %get-tuple-element.663) | copy-start | bytes 466948 | tf_op jit(solution)/shard_map/while
  237.8 12.6 %copy-start.14 = (bf16[128,576]{1,0:T(8,128)(2,1)S(1)}, bf16[128,576]{1,0:T(8,128)(2,1)}, u32[]{:S(2)}) copy-start(bf16[128,576]{1,0:T(8,128)(2,1)} %get-tuple-element.668) | copy-start | bytes 442372 | tf_op jit(solution)/shard_map/while
  237.8 12.6 %copy-start.16 = (bf16[128,544]{1,0:T(8,128)(2,1)S(1)}, bf16[128,544]{1,0:T(8,128)(2,1)}, u32[]{:S(2)}) copy-start(bf16[128,544]{1,0:T(8,128)(2,1)} %get-tuple-element.667) | copy-start | bytes 417796 | tf_op jit(solution)/shard_map/while
  277.2 50.1 %copy-start.1 = (bf16[1536,1024]{1,0:T(8,128)(2,1)S(1)}, bf16[1536,1024]{1,0:T(8,128)(2,1)}, u32[]{:S(2)}) copy-start(bf16[1536,1024]{1,0:T(8,128)(2,1)} %get-tuple-element.1109) | copy-start | bytes 9437188
  353.9 10.0 %copy-start.7 = (bf16[128,704]{1,0:T(8,128)(2,1)S(1)}, bf16[128,704]{1,0:T(8,128)(2,1)}, u32[]{:S(2)}) copy-start(bf16[128,704]{1,0:T(8,128)(2,1)} %get-tuple-element.729) | copy-start | bytes 540676 | tf_op jit(solution)/shard_map/while
  353.9 10.0 %copy-start.9 = (bf16[128,672]{1,0:T(8,128)(2,1)S(1)}, bf16[128,672]{1,0:T(8,128)(2,1)}, u32[]{:S(2)}) copy-start(bf16[128,672]{1,0:T(8,128)(2,1)} %get-tuple-element.728) | copy-start | bytes 516100 | tf_op jit(solution)/shard_map/while
  353.9 11.5 %copy-start.19 = (bf16[128,640]{1,0:T(8,128)(2,1)S(1)}, bf16[128,640]{1,0:T(8,128)(2,1)}, u32[]{:S(2)}) copy-start(bf16[128,640]{1,0:T(8,128)(2,1)} %get-tuple-element.733) | copy-start | bytes 491524 | tf_op jit(solution)/shard_map/while
  353.9 11.5 %copy-start.21 = (bf16[128,608]{1,0:T(8,128)(2,1)S(1)}, bf16[128,608]{1,0:T(8,128)(2,1)}, u32[]{:S(2)}) copy-start(bf16[128,608]{1,0:T(8,128)(2,1)} %get-tuple-element.732) | copy-start | bytes 466948 | tf_op jit(solution)/shard_map/while
  354.2 12.6 %copy-start.15 = (bf16[128,576]{1,0:T(8,128)(2,1)S(1)}, bf16[128,576]{1,0:T(8,128)(2,1)}, u32[]{:S(2)}) copy-start(bf16[128,576]{1,0:T(8,128)(2,1)} %get-tuple-element.737) | copy-start | bytes 442372 | tf_op jit(solution)/shard_map/while
  354.2 12.6 %copy-start.17 = (bf16[128,544]{1,0:T(8,128)(2,1)S(1)}, bf16[128,544]{1,0:T(8,128)(2,1)}, u32[]{:S(2)}) copy-start(bf16[128,544]{1,0:T(8,128)(2,1)} %get-tuple-element.736) | copy-start | bytes 417796 | tf_op jit(solution)/shard_map/while
  399.6 10.0 %copy-start.7 = (bf16[128,704]{1,0:T(8,128)(2,1)S(1)}, bf16[128,704]{1,0:T(8,128)(2,1)}, u32[]{:S(2)}) copy-start(bf16[128,704]{1,0:T(8,128)(2,1)} %get-tuple-element.729) | copy-start | bytes 540676 | tf_op jit(solution)/shard_map/while
  399.6 10.0 %copy-start.9 = (bf16[128,672]{1,0:T(8,128)(2,1)S(1)}, bf16[128,672]{1,0:T(8,128)(2,1)}, u32[]{:S(2)}) copy-start(bf16[128,672]{1,0:T(8,128)(2,1)} %get-tuple-element.728) | copy-start | bytes 516100 | tf_op jit(solution)/shard_map/while
  399.6 11.5 %copy-start.19 = (bf16[128,640]{1,0:T(8,128)(2,1)S(1)}, bf16[128,640]{1,0:T(8,128)(2,1)}, u32[]{:S(2)}) copy-start(bf16[128,640]{1,0:T(8,128)(2,1)} %get-tuple-element.733) | copy-start | bytes 491524 | tf_op jit(solution)/shard_map/while
  399.7 11.5 %copy-start.21 = (bf16[128,608]{1,0:T(8,128)(2,1)S(1)}, bf16[128,608]{1,0:T(8,128)(2,1)}, u32[]{:S(2)}) copy-start(bf16[128,608]{1,0:T(8,128)(2,1)} %get-tuple-element.732) | copy-start | bytes 466948 | tf_op jit(solution)/shard_map/while
  400.0 12.6 %copy-start.15 = (bf16[128,576]{1,0:T(8,128)(2,1)S(1)}, bf16[128,576]{1,0:T(8,128)(2,1)}, u32[]{:S(2)}) copy-start(bf16[128,576]{1,0:T(8,128)(2,1)} %get-tuple-element.737) | copy-start | bytes 442372 | tf_op jit(solution)/shard_map/while
  400.0 12.6 %copy-start.17 = (bf16[128,544]{1,0:T(8,128)(2,1)S(1)}, bf16[128,544]{1,0:T(8,128)(2,1)}, u32[]{:S(2)}) copy-start(bf16[128,544]{1,0:T(8,128)(2,1)} %get-tuple-element.736) | copy-start | bytes 417796 | tf_op jit(solution)/shard_map/while
  445.4 10.0 %copy-start.7 = (bf16[128,704]{1,0:T(8,128)(2,1)S(1)}, bf16[128,704]{1,0:T(8,128)(2,1)}, u32[]{:S(2)}) copy-start(bf16[128,704]{1,0:T(8,128)(2,1)} %get-tuple-element.729) | copy-start | bytes 540676 | tf_op jit(solution)/shard_map/while
  445.4 10.0 %copy-start.9 = (bf16[128,672]{1,0:T(8,128)(2,1)S(1)}, bf16[128,672]{1,0:T(8,128)(2,1)}, u32[]{:S(2)}) copy-start(bf16[128,672]{1,0:T(8,128)(2,1)} %get-tuple-element.728) | copy-start | bytes 516100 | tf_op jit(solution)/shard_map/while
  445.4 11.5 %copy-start.19 = (bf16[128,640]{1,0:T(8,128)(2,1)S(1)}, bf16[128,640]{1,0:T(8,128)(2,1)}, u32[]{:S(2)}) copy-start(bf16[128,640]{1,0:T(8,128)(2,1)} %get-tuple-element.733) | copy-start | bytes 491524 | tf_op jit(solution)/shard_map/while
  445.4 11.5 %copy-start.21 = (bf16[128,608]{1,0:T(8,128)(2,1)S(1)}, bf16[128,608]{1,0:T(8,128)(2,1)}, u32[]{:S(2)}) copy-start(bf16[128,608]{1,0:T(8,128)(2,1)} %get-tuple-element.732) | copy-start | bytes 466948 | tf_op jit(solution)/shard_map/while
  445.7 12.6 %copy-start.15 = (bf16[128,576]{1,0:T(8,128)(2,1)S(1)}, bf16[128,576]{1,0:T(8,128)(2,1)}, u32[]{:S(2)}) copy-start(bf16[128,576]{1,0:T(8,128)(2,1)} %get-tuple-element.737) | copy-start | bytes 442372 | tf_op jit(solution)/shard_map/while
  445.7 12.6 %copy-start.17 = (bf16[128,544]{1,0:T(8,128)(2,1)S(1)}, bf16[128,544]{1,0:T(8,128)(2,1)}, u32[]{:S(2)}) copy-start(bf16[128,544]{1,0:T(8,128)(2,1)} %get-tuple-element.736) | copy-start | bytes 417796 | tf_op jit(solution)/shard_map/while
  491.1 10.0 %copy-start.7 = (bf16[128,704]{1,0:T(8,128)(2,1)S(1)}, bf16[128,704]{1,0:T(8,128)(2,1)}, u32[]{:S(2)}) copy-start(bf16[128,704]{1,0:T(8,128)(2,1)} %get-tuple-element.729) | copy-start | bytes 540676 | tf_op jit(solution)/shard_map/while
  491.1 10.0 %copy-start.9 = (bf16[128,672]{1,0:T(8,128)(2,1)S(1)}, bf16[128,672]{1,0:T(8,128)(2,1)}, u32[]{:S(2)}) copy-start(bf16[128,672]{1,0:T(8,128)(2,1)} %get-tuple-element.728) | copy-start | bytes 516100 | tf_op jit(solution)/shard_map/while
  491.1 11.5 %copy-start.19 = (bf16[128,640]{1,0:T(8,128)(2,1)S(1)}, bf16[128,640]{1,0:T(8,128)(2,1)}, u32[]{:S(2)}) copy-start(bf16[128,640]{1,0:T(8,128)(2,1)} %get-tuple-element.733) | copy-start | bytes 491524 | tf_op jit(solution)/shard_map/while
  491.1 11.5 %copy-start.21 = (bf16[128,608]{1,0:T(8,128)(2,1)S(1)}, bf16[128,608]{1,0:T(8,128)(2,1)}, u32[]{:S(2)}) copy-start(bf16[128,608]{1,0:T(8,128)(2,1)} %get-tuple-element.732) | copy-start | bytes 466948 | tf_op jit(solution)/shard_map/while
  491.4 12.6 %copy-start.15 = (bf16[128,576]{1,0:T(8,128)(2,1)S(1)}, bf16[128,576]{1,0:T(8,128)(2,1)}, u32[]{:S(2)}) copy-start(bf16[128,576]{1,0:T(8,128)(2,1)} %get-tuple-element.737) | copy-start | bytes 442372 | tf_op jit(solution)/shard_map/while
  491.5 12.6 %copy-start.17 = (bf16[128,544]{1,0:T(8,128)(2,1)S(1)}, bf16[128,544]{1,0:T(8,128)(2,1)}, u32[]{:S(2)}) copy-start(bf16[128,544]{1,0:T(8,128)(2,1)} %get-tuple-element.736) | copy-start | bytes 417796 | tf_op jit(solution)/shard_map/while
  (28 other events, 209.8 us)
Sparse Core Ops, SparseCore 0:
  39.3 14.3 all-gather.2
  259.3 10.2 all-gather.4
